TPU v7x, 32 devices: a whole 2x2x4 slice. The times are simulated.
32 devices in a mesh: dev: 16 (over z, y, x), rep: 2 (over core).
Axes of the slice: x: 2, y: 2, z: 4, core: 2. Of those that a mesh axis runs over, the one named last changes fastest.
Arguments:
- embeddings: float32 [4096, 4096], P(('rep', 'dev')), parts along dimension 0, may hold values from -130 to 130
- cluster_id: int32 [4096], P(('rep', 'dev')), parts along dimension 0, may hold values from 0 to 31, as said below
- member_order: int32 [4096], P(('rep', 'dev')), parts along dimension 0, may hold values from 0 to 127, as said below
- cluster_slot: int32 [64], P('rep'), parts along dimension 0, may hold values from 0 to 31, each once
- cluster_size: int32 [64], P('rep'), parts along dimension 0, may hold values from 16 to 128, as said below
Outputs:
- best_similarity: float32 [4096], P(('rep', 'dev')), parts along dimension 0
- keep: int32 [4096], P(('rep', 'dev')), parts along dimension 0
- cluster_mean: float32 [64], P(('rep', 'dev')), parts along dimension 0
There are 2 independent parts, one for each index of `rep`. A program takes and returns all parts, laid end to end along the dimension named above; each array names one. Nothing has to cross between parts.
Inputs may be any that keep to these rules, and one draw needn't show every extreme that they name: `cluster_id`: every cluster holds at most 128 rows and some cluster exactly 128. A cluster of n members has floor(n / 16) or ceil(n / 16) of them among the rows of each device, so at most 8, a number reached on every device. `member_order`: within a cluster of n members the ranks are 0 to n - 1, each once. `cluster_slot`: a permutation; cluster c is owned by device cluster_slot[c] // 2 of dev. `cluster_size`: the number of rows whose cluster_id is c.
All inputs are finite; a program needn't handle non-finite values.
Results may differ from a plain program's by a relative error of at most 0.0003.
Values may be sent and summed in bfloat16 or wider, within the bound.
A program may use at most 64 MiB of HBM per device.

v0:
```python
import functools

import jax
import jax.numpy as jnp
from jax import lax
from jax.experimental import pallas as pl
from jax.experimental.pallas import tpu as pltpu
from jax.sharding import PartitionSpec as P

CAP = 128
CHUNK = 128
LOADS = 4
LAG = 2
NORM_EPS = 1e-06
CUTOFF = 0.8
F32 = jnp.float32
BF16 = jnp.bfloat16
I32 = jnp.int32


def split_lines(n):
    z = max(z for z in range(1, n + 1) if n % z == 0 and z * z <= n)
    return z, n // z


def line_slots(n, nz, nq, rows, group):
    largest = rows * n // nq + CAP - CAP // nq
    bound = -(-largest // nq) + -(-group * nz * (n - 1) // n)
    return min(group * (CAP // nq), -(-bound // 16) * 16)


def iota(shape, dim):
    return lax.broadcasted_iota(I32, shape, dim)


def rows_of(values, width):
    row = iota((8, width), 0)
    out = jnp.zeros((8, width), values[0].dtype)
    for r, v in enumerate(values):
        out = jnp.where(row == r, jnp.broadcast_to(v, (8, width)), out)
    return out


def to_col(row, count):
    eye = iota((count, count), 0) == iota((count, count), 1)
    return jnp.sum(jnp.where(eye, row, 0.0), axis=1, keepdims=True)


def floor_div(x, d):
    return jnp.floor((x + 0.5) * (1.0 / d))


def kernel(n, nz, nq, emb_hbm, cid, order, slot, size, packed_out,
           emb, s_load, unit, line, meta, place, pick, packed, plane, ots, otr, gram, hs, hr, table, units, repack, labs,
           s_meta, r_meta, s_line, r_line, s_plane, r_plane, s_ot, r_ot, s_h, r_h, s_t, r_t):
    me = lax.axis_index("dev")
    parts = s_load.shape[0]
    tall = emb.shape[0] // parts
    loads = [pltpu.make_async_copy(emb_hbm.at[pl.ds(i * tall, tall)], emb.at[pl.ds(i * tall, tall)],
                                   s_load.at[i]) for i in range(parts)]
    for c in loads:
        c.start()
    z, q = lax.div(me, nq), lax.rem(me, nq)
    rows = emb.shape[0]
    clusters = slot.shape[1]
    per_owner = clusters // n
    chunks, width = unit.shape[1], unit.shape[3]
    group = nz * per_owner
    seg = CAP // nq
    slots = pick.shape[1]
    half = CAP // 2

    def copy(src, dst, s, r, target):
        return pltpu.make_async_remote_copy(
            src_ref=src, dst_ref=dst, send_sem=s, recv_sem=r,
            device_id={"dev": target}, device_id_type=pl.DeviceIdType.MESH)

    def on_line(d):
        return lax.rem(z + d, nz)

    def on_plane(d):
        return lax.rem(q + d, nq)

    barrier = pltpu.get_barrier_semaphore()
    friends = [on_line(d) * nq + q for d in range(1, nz)] + [z * nq + on_plane(d) for d in range(1, nq)]
    for t in friends:
        pl.semaphore_signal(barrier, inc=1, device_id={"dev": t},
                            device_id_type=pl.DeviceIdType.MESH)

    meta[z] = rows_of([cid[...], order[...]], rows)
    sums = []
    for i in range(parts):
        loads[i].wait()
        x = emb[i * tall:(i + 1) * tall, :]
        sums.append(jnp.sum(x * x, axis=1, keepdims=True))
    scale = lax.rsqrt(jnp.concatenate(sums, axis=0) + NORM_EPS)
    pl.semaphore_wait(barrier, len(friends))

    metas = [copy(meta.at[z], meta.at[z], s_meta.at[d], r_meta.at[d], on_line(d) * nq + q)
             for d in range(1, nz)]
    for c in metas:
        c.start()
    lines = []
    for k in range(chunks):
        for t in range(nz):
            c0 = (t * chunks + k) * width
            unit[t, k] = (emb[:, c0:c0 + width] * scale).astype(BF16)
        now = [copy(unit.at[on_line(d), k], line.at[k, z], s_line.at[k, d], r_line.at[k, d],
                    on_line(d) * nq + q) for d in range(nz - 1, 0, -1)]
        for c in now:
            c.start()
        line[k, z] = unit[z, k]
        lines.append(now)

    slot_c = to_col(slot[...].astype(F32), clusters)
    size_c = to_col(size[...].astype(F32), clusters)
    size_r = size[...].astype(F32)
    c_row, c_col = iota((clusters, clusters), 1), iota((clusters, clusters), 0)
    ahead = (size_r > size_c) | ((size_r == size_c) & (c_row < c_col))
    place_in = jnp.sum(jnp.where(ahead, 1.0, 0.0), axis=1, keepdims=True)
    e_c = floor_div(place_in, nq)
    turn = place_in - e_c * nq
    odd = e_c - 2.0 * floor_div(e_c, 2)
    g_c = jnp.where(odd > 0.5, nq - 1 - turn, turn)
    oz_c = floor_div(e_c, per_owner)
    local_c = e_c - oz_c * per_owner
    work_c = (oz_c * nq + g_c) * per_owner + local_c
    for c in metas:
        c.wait_recv()
    tri = (iota((rows, rows), 0) < iota((rows, rows), 1)).astype(F32).astype(BF16)
    counts = jnp.zeros((clusters, 1), F32)
    for b in range(nz):
        mem = jnp.where(iota((clusters, rows), 0) == meta[b, 0:1, :], 1.0, 0.0)
        counts = counts + jnp.sum(mem, axis=1, keepdims=True)
    eye = c_row == c_col
    g_r = jnp.sum(jnp.where(eye, g_c, 0.0), axis=0, keepdims=True)
    e_r = jnp.sum(jnp.where(eye, e_c, 0.0), axis=0, keepdims=True)
    n_r = jnp.sum(jnp.where(eye, counts, 0.0), axis=0, keepdims=True)
    first = (g_r == g_c) & (e_r < e_c)
    place_c = g_c * slots + jnp.sum(jnp.where(first, n_r, 0.0), axis=1, keepdims=True)
    base = jnp.zeros((clusters, 1), F32)
    for b in range(nz):
        is_mem = iota((clusters, rows), 0) == meta[b, 0:1, :]
        mem = is_mem.astype(F32)
        before = base + jnp.dot(mem.astype(BF16), tri, preferred_element_type=F32)

        def of_row(v):
            return jnp.sum(jnp.where(is_mem, v, 0.0), axis=0, keepdims=True)

        rank = of_row(before)
        vals = [of_row(place_c) + rank, rank + (q * seg).astype(F32), of_row(work_c),
                meta[b, 1:2, :].astype(F32) + 1.0, of_row(e_c) + 1.0]
        place[:, b * rows:(b + 1) * rows] = rows_of(vals, rows)
        base = base + jnp.sum(mem, axis=1, keepdims=True)

    all_rows = nz * rows
    place_i = place[0:1, :].astype(I32)
    label_row = iota((8, all_rows), 0)
    small = (label_row == 1) | (label_row == 3) | (label_row == 4)
    labels = jnp.where(small, place[...], 0.0).astype(BF16)

    def make_pick(t, _):
        hit = iota((slots, all_rows), 0) + t * slots == place_i
        pick[t] = jnp.where(hit, 1.0, 0.0).astype(BF16)
        ots[t] = lax.dot_general(labels, pick[t], (((1,), (1,)), ((), ())),
                                 preferred_element_type=F32)
        return 0

    lax.fori_loop(0, nq, make_pick, 0)
    otr[q] = ots[q]
    orders = [copy(ots.at[on_plane(d)], otr.at[q], s_ot.at[d], r_ot.at[d], z * nq + on_plane(d))
              for d in range(1, nq)]
    for c in orders:
        c.start()

    below = iota((half, CAP), 0) + half > iota((half, CAP), 1)

    def spread(k):
        for c in planes[k]:
            c.wait_recv()
        got = jnp.dot(repack[...].reshape(group * CAP, nq * slots),
                      plane[k].reshape(nq * slots, width), preferred_element_type=F32)
        units[...] = got.astype(BF16).reshape(group, CAP, width)

    def partial_gram(e):
        m = units[e]
        return lax.dot_general(m, m, (((1,), (1,)), ((), ())), preferred_element_type=F32)

    def add_gram(k):
        if k == 0:
            make_repack()
        spread(k)
        for e in range(group):
            s = partial_gram(e)
            gram[e] = s if k == 0 else gram[e] + s

    def make_repack():
        for c in orders:
            c.wait_recv()
        for t in range(nq):
            labs[:, t * slots:(t + 1) * slots] = otr[t]
        target = ((labs[4:5, :] - 1.0) * CAP + labs[1:2, :]).astype(I32)

        def one(e, _):
            hit = iota((CAP, nq * slots), 0) + e * CAP == target
            repack[e] = jnp.where(hit, 1.0, 0.0).astype(BF16)
            return 0

        lax.fori_loop(0, group, one, 0)

    planes = []
    for k in range(chunks):
        for c in lines[k]:
            c.wait_recv()
        block = line[k].reshape(all_rows, width)
        now = []
        for d in list(range(1, nq)) + [0]:
            t = on_plane(d)
            got = jnp.dot(pick[t], block, preferred_element_type=F32).astype(BF16)
            if d == 0:
                plane[k, q] = got
            else:
                packed[k, t] = got
                c = copy(packed.at[k, t], plane.at[k, q], s_plane.at[k, d], r_plane.at[k, d],
                         z * nq + t)
                c.start()
                now.append(c)
        planes.append(now)
        if k >= LAG:
            add_gram(k - LAG)

    for k in range(max(chunks - LAG, 0), chunks - 1):
        add_gram(k)
    if chunks == 1:
        make_repack()
    spread(chunks - 1)
    halves = []
    for d in list(range(1, nz)) + [0]:
        t = on_line(d)
        for l in range(per_owner):
            full = partial_gram(t * per_owner + l)
            if chunks > 1:
                full = full + gram[t * per_owner + l]
            hs[t, l] = jnp.where(below, full[half:, :], pltpu.roll(full[:half, :], half, 1))
        if d:
            c = copy(hs.at[t], hr.at[z], s_h.at[d], r_h.at[d], t * nq + q)
            c.start()
            halves.append(c)
    hr[z] = hs[z]
    ranks = labs[...].astype(BF16)
    ord_rows = []
    for l in range(per_owner):
        r = lax.dot_general(ranks, repack[z * per_owner + l], (((1,), (1,)), ((), ())),
                            preferred_element_type=F32)
        ord_rows.append(r[3:4, :])
    ord_r = rows_of(ord_rows, CAP)
    ord_cols = ord_r.T
    for c in halves:
        c.wait_recv()
    bests, means = [], []
    up = iota((half, half), 0) < iota((half, half), 1)
    down = iota((half, half), 0) > iota((half, half), 1)
    for l in range(per_owner):
        p = hr[0, l]
        for t in range(1, nz):
            p = p + hr[t, l]
        pt = p.T
        u, ut = p[:, half:], pt[half:, :]
        top = jnp.concatenate([jnp.where(up, u, ut), pt[:half, :]], axis=1)
        bottom = jnp.concatenate([p[:, :half], jnp.where(down, u, ut)], axis=1)
        sim = jnp.concatenate([top, bottom], axis=0)
        mine = (me * per_owner + l).astype(F32)
        n_mem = jnp.sum(jnp.where(work_c == mine, size_c, 0.0), axis=0, keepdims=True)
        o_row, o_col = ord_r[l:l + 1, :], ord_cols[:, l:l + 1]
        ok = (o_col < o_row) & (o_col >= 1.0) & (o_col <= n_mem)
        near = jnp.max(jnp.where(ok, sim, -1.0), axis=0, keepdims=True)
        live = (o_row >= 1.0) & (o_row <= n_mem)
        bests.append(jnp.where(live, near, -1.0))
        means.append(jnp.sum(jnp.where(live, near, 0.0), axis=1, keepdims=True) / n_mem)
    lanes = jnp.zeros((1, CAP), F32)
    for l in range(per_owner):
        lanes = jnp.where(iota((1, CAP), 1) == l, means[l], lanes)
    table[me] = rows_of(bests + [lanes], CAP)[:table.shape[1], :]
    backs = [copy(table.at[me], table.at[me], s_t.at[d], r_t.at[d], lax.rem(me + d, n))
             for d in range(1, n)]
    for c in backs:
        c.start()
    own = pl.ds(pl.multiple_of(z * rows, rows), rows)
    s8 = place[2:3, own].astype(I32)
    pos = place[1:2, own].astype(I32)
    hot = jnp.where(iota((clusters, rows), 0) == s8, 1.0, 0.0)
    for c in backs:
        c.wait_recv()
    full = table[...]
    flat = full[:, :per_owner, :].reshape(clusters, CAP).T
    told = full[:, per_owner:per_owner + 1, :].reshape(n, CAP)
    mean = jnp.zeros((1, rows), F32)
    for l in range(per_owner):
        own_slot = (me * per_owner + l).astype(F32)
        work = jnp.sum(jnp.where(slot_c == own_slot, work_c, 0.0), axis=0, keepdims=True).astype(I32)
        hit = iota((n, CAP), 0) * per_owner + iota((n, CAP), 1) == work
        hit = hit & (iota((n, CAP), 1) < per_owner)
        part = jnp.sum(jnp.where(hit, told, 0.0), axis=1, keepdims=True)
        mean = jnp.where(iota((1, rows), 1) == l, jnp.sum(part, axis=0, keepdims=True), mean)
    got = jnp.dot(flat, hot, preferred_element_type=F32, precision=lax.Precision.HIGHEST)
    out = jnp.sum(jnp.where(iota((CAP, rows), 0) == pos, got, 0.0), axis=0, keepdims=True)
    packed_out[...] = rows_of([out, mean], rows)
    for group_of in [metas, orders, halves, backs] + lines + planes:
        for c in group_of:
            c.wait_send()


def finish(packed, best_out, keep_out, mean_out):
    best = packed[0:1, :]
    best_out[...] = best
    keep_out[...] = jnp.where(best < CUTOFF, 1, 0)
    mean_out[...] = packed[1:2, :mean_out.shape[1]]


def body(embeddings, cluster_id, member_order, cluster_slot, cluster_size):
    n = lax.axis_size("dev")
    nz, nq = split_lines(n)
    rows, depth = embeddings.shape
    clusters = cluster_slot.shape[0]
    per_owner = clusters // n
    width = min(CHUNK, depth // nz)
    chunks = depth // nz // width
    group = nz * per_owner
    slots = line_slots(n, nz, nq, rows, group)
    vmem = pl.BlockSpec(memory_space=pltpu.VMEM)
    dma = pltpu.SemaphoreType.DMA
    packed = pl.pallas_call(
        functools.partial(kernel, n, nz, nq),
        out_shape=jax.ShapeDtypeStruct((8, rows), F32),
        in_specs=[pl.BlockSpec(memory_space=pl.ANY)] + [vmem] * 4,
        out_specs=vmem,
        scratch_shapes=[
            pltpu.VMEM((rows, depth), F32),
            dma((LOADS,)),
            pltpu.VMEM((nz, chunks, rows, width), BF16),
            pltpu.VMEM((chunks, nz, rows, width), BF16),
            pltpu.VMEM((nz, 8, rows), I32),
            pltpu.VMEM((8, nz * rows), F32),
            pltpu.VMEM((nq, slots, nz * rows), BF16),
            pltpu.VMEM((chunks, nq, slots, width), BF16),
            pltpu.VMEM((chunks, nq, slots, width), BF16),
            pltpu.VMEM((nq, 8, slots), F32),
            pltpu.VMEM((nq, 8, slots), F32),
            pltpu.VMEM((group, CAP, CAP), F32),
            pltpu.VMEM((nz, per_owner, CAP // 2, CAP), F32),
            pltpu.VMEM((nz, per_owner, CAP // 2, CAP), F32),
            pltpu.VMEM((n, pl.next_power_of_2(per_owner + 1), CAP), F32),
            pltpu.VMEM((group, CAP, width), BF16),
            pltpu.VMEM((group, CAP, nq * slots), BF16),
            pltpu.VMEM((8, nq * slots), F32),
            dma((nz,)), dma((nz,)),
            dma((chunks, nz)), dma((chunks, nz)),
            dma((chunks, nq)), dma((chunks, nq)),
            dma((nq,)), dma((nq,)),
            dma((nz,)), dma((nz,)),
            dma((n,)), dma((n,)),
        ],
        compiler_params=pltpu.CompilerParams(
            collective_id=0, has_side_effects=True, vmem_limit_bytes=60 * 1024 * 1024),
    )(embeddings, cluster_id.reshape(1, rows), member_order.reshape(1, rows),
      cluster_slot.reshape(1, clusters), cluster_size.reshape(1, clusters))
    best, keep, mean = pl.pallas_call(
        finish,
        out_shape=(jax.ShapeDtypeStruct((1, rows), F32), jax.ShapeDtypeStruct((1, rows), I32),
                   jax.ShapeDtypeStruct((1, per_owner), F32)),
        in_specs=[vmem],
        out_specs=(vmem,) * 3,
    )(packed)
    return best.reshape(rows), keep.reshape(rows), mean.reshape(per_owner)


def solution(mesh):
    placed = (P(("rep", "dev"), None), P(("rep", "dev")), P(("rep", "dev")), P("rep"), P("rep"))
    return jax.shard_map(
        body,
        mesh=mesh,
        in_specs=placed,
        out_specs=(P(("rep", "dev")), P(("rep", "dev")), P(("rep", "dev"))),
        check_vma=False,
    )
```

profile of v0, /device:TPU:0, one launch (start us, length us, event | category | flops | bytes accessed | tf_op | source)
XLA Modules:
  0.0 54.1 jit_solution(11651562035436768208)
XLA Ops:
  0.6 52.3 %shard_map.76.packed = f32[8,128]{1,0:T(8,128)} custom-call(f32[128,4096]{1,0:T(8,128)} %emb_hbm.1, s32[1,128]{1,0:T(1,128)} %bitcast.7, s32[1,128]{1,0:T(1,128)} %bitcast.8, s32[1,32]{1,0:T(1,128)} %bitcast.9, s32[1,32]{1,0:T(1,128)} %bitcast.10), custom_call_target="tpu_custom_call" | custom-call | tf_op jit(solution)/shard_map/pallas_call | solution.py:332
  52.9 1.2 %shard_map.77 = (f32[1,128]{1,0:T(1,128)}, s32[1,128]{1,0:T(1,128)}, f32[1,2]{1,0:T(1,128)}) custom-call(f32[8,128]{1,0:T(8,128)} %shard_map.76.packed), custom_call_target="tpu_custom_call" | custom-call | tf_op jit(solution)/shard_map/pallas_call | solution.py:367
where the time goes:
time: 54.3 us; the launch traced here: 54.1 us
  Pallas kernels  53.5 us (99%)
  between operations  0.64 us (1%)
    pallas_call x1, Pallas kernels, body(): pl.pallas_call(functools.partial(kernel, n, nz, nq), out_shape=jax.ShapeD...  52.3 us
    pallas_call x1, Pallas kernels, body(): pl.pallas_call(finish, out_shape=(jax.ShapeDtypeStruct((1, rows), F32), j...  1.19 us

commit v1 on v0

v1 whole, which is shorter than its diff:
```python
import functools

import jax
import jax.numpy as jnp
from jax import lax
from jax.experimental import pallas as pl
from jax.experimental.pallas import tpu as pltpu
from jax.sharding import PartitionSpec as P

CAP = 128
CHUNK = 128
LOADS = 4
WINDOW = 3
LAG = 2
DIRECT = 1
NORM_EPS = 1e-06
CUTOFF = 0.8
FIXED = 32000.0
F32 = jnp.float32
BF16 = jnp.bfloat16
I16 = jnp.int16
I32 = jnp.int32


def split_lines(n):
    z = max(z for z in range(1, n + 1) if n % z == 0 and z * z <= n)
    return z, n // z


def source_slots(n, nq, rows, group):
    largest = rows * n // nq + CAP - CAP // nq
    bound = (largest + group * (n - 1)) // n
    return min(group * -(-CAP // n), -(-bound // 16) * 16)


def iota(shape, dim):
    return lax.broadcasted_iota(I32, shape, dim)


def rows_of(values, width):
    row = iota((8, width), 0)
    out = jnp.zeros((8, width), values[0].dtype)
    for r, v in enumerate(values):
        out = jnp.where(row == r, jnp.broadcast_to(v, (8, width)), out)
    return out


def to_col(row, count):
    eye = iota((count, count), 0) == iota((count, count), 1)
    return jnp.sum(jnp.where(eye, row, 0.0), axis=1, keepdims=True)


def floor_div(x, d):
    return jnp.floor((x + 0.5) * (1.0 / d))


def kernel(n, nz, nq, emb_hbm, cid_hbm, order_hbm, slot_hbm, size_hbm, packed_out,
           emb, cid, order, slot, size, unit, line, meta, pick, packed, plane, straight, ots, otr,
           gram, own_half, hs, hr, table, units, repack,
           s_load, s_small, s_meta, r_meta, s_line, r_line, s_plane, r_plane, s_dir, r_dir,
           s_ot, r_ot, s_h, r_h, s_t, r_t):
    me = lax.axis_index("dev")
    z, q = lax.div(me, nq), lax.rem(me, nq)

    def copy(src, dst, s, r, target):
        return pltpu.make_async_remote_copy(
            src_ref=src, dst_ref=dst, send_sem=s, recv_sem=r,
            device_id={"dev": target}, device_id_type=pl.DeviceIdType.MESH)

    def on_line(d):
        return jnp.bitwise_xor(z, d) * nq + q

    def on_plane(d):
        return z * nq + jnp.bitwise_xor(q, d)

    barrier = pltpu.get_barrier_semaphore()
    friends = [on_line(d) for d in range(1, nz)] + [on_plane(d) for d in range(1, nq)]
    for t in friends:
        pl.semaphore_signal(barrier, inc=1, device_id={"dev": t},
                            device_id_type=pl.DeviceIdType.MESH)
    smalls = [pltpu.make_async_copy(a, b, s_small.at[i]) for i, (a, b) in enumerate(
        [(cid_hbm, cid), (order_hbm, order), (slot_hbm, slot), (size_hbm, size)])]
    parts = s_load.shape[0]
    tall = emb.shape[0] // parts
    loads = [pltpu.make_async_copy(emb_hbm.at[pl.ds(i * tall, tall)], emb.at[pl.ds(i * tall, tall)],
                                   s_load.at[i]) for i in range(parts)]
    for c in smalls + loads:
        c.start()
    rows = emb.shape[0]
    clusters = slot.shape[1]
    per_owner = clusters // n
    chunks, width = line.shape[0], line.shape[3]
    group = nz * per_owner
    slots = plane.shape[2] // nz
    half = CAP // 2
    lined = chunks - DIRECT

    for c in smalls:
        c.wait()
    slot_c = to_col(slot[...].astype(F32), clusters)
    size_r = size[...].astype(F32)
    size_c = to_col(size_r, clusters)
    c_row, c_col = iota((clusters, clusters), 1), iota((clusters, clusters), 0)
    ahead = (size_r > size_c) | ((size_r == size_c) & (c_row < c_col))
    place_in = jnp.sum(jnp.where(ahead, 1.0, 0.0), axis=1, keepdims=True)
    e_c = floor_div(place_in, nq)
    turn = place_in - e_c * nq
    odd = e_c - 2.0 * floor_div(e_c, 2)
    g_c = jnp.where(odd > 0.5, nq - 1 - turn, turn)
    oz_c = floor_div(e_c, per_owner)
    local_c = e_c - oz_c * per_owner
    work_c = (oz_c * nq + g_c) * per_owner + local_c
    is_mem = iota((clusters, rows), 0) == cid[...]

    def of_row(v):
        return jnp.sum(jnp.where(is_mem, v, 0.0), axis=0, keepdims=True)

    e_row, work_row = of_row(e_c), of_row(work_c).astype(I32)
    rel = jnp.bitwise_xor(of_row(g_c).astype(I32), q)
    tri = (iota((rows, rows), 0) < iota((rows, rows), 1)).astype(F32).astype(BF16)
    wide_q = -(-nq // 16) * 16
    in_group = iota((wide_q, rows), 0) == rel
    before = jnp.dot(in_group.astype(F32).astype(BF16), tri, preferred_element_type=F32)
    rank = jnp.sum(jnp.where(in_group, before, 0.0), axis=0, keepdims=True)
    place = rel.astype(F32) * slots + rank
    ord_row = order[...].astype(F32)
    meta[0] = rows_of([place, ord_row + 1.0, e_row + 1.0], rows)

    sums = []
    for i in range(parts):
        loads[i].wait()
        x = emb[i * tall:(i + 1) * tall, :]
        sums.append(jnp.sum(x * x, axis=1, keepdims=True))
    scale = lax.rsqrt(jnp.concatenate(sums, axis=0) + NORM_EPS)

    lines, planes = [], []
    line_order = [d for d in (2, 3, 1) if d < nz] + list(range(4, nz))

    def make_unit(k):
        for t in range(nz):
            c0 = (t * chunks + k) * width
            unit[t, k] = (emb[:, c0:c0 + width] * scale).astype(BF16)

    def send_line(k):
        make_unit(k)
        now = [copy(unit.at[jnp.bitwise_xor(z, d), k], line.at[k, d], s_line.at[k, d], r_line.at[k, d], on_line(d))
               for d in line_order]
        for c in now:
            c.start()
        line[k, 0] = unit[z, k]
        lines.append(now)

    pl.semaphore_wait(barrier, len(friends))
    metas = [copy(meta.at[0], meta.at[d], s_meta.at[d], r_meta.at[d], on_line(d)) for d in range(1, nz)]
    for c in metas:
        c.start()
    for k in range(min(WINDOW, lined)):
        send_line(k)

    def label(d):
        pick[d] = jnp.where(iota((nq * slots, rows), 0) == meta[d, 0:1, :].astype(I32), 1.0, 0.0).astype(BF16)
        values = jnp.where((iota((8, rows), 0) == 1) | (iota((8, rows), 0) == 2), meta[d], 0.0).astype(BF16)
        return lax.dot_general(values, pick[d], (((1,), (1,)), ((), ())), preferred_element_type=F32)

    told = [label(0)]
    if DIRECT:
        make_unit(chunks - 1)
        for t in range(nz):
            got = jnp.dot(pick[0], unit[t, chunks - 1], preferred_element_type=F32).astype(BF16)
            straight[t] = got.reshape(nq, slots, width)
        plane[chunks - 1, 0, 0:slots] = straight[z, 0]
    for d, c in enumerate(metas):
        c.wait_recv()
        told.append(label(d + 1))
    for d in range(nq):
        ots[d] = jnp.concatenate([v[:, d * slots:(d + 1) * slots] for v in told], axis=1)
    orders = [copy(ots.at[d], otr.at[d], s_ot.at[d], r_ot.at[d], on_plane(d)) for d in range(1, nq)]
    for c in orders:
        c.start()

    def make_repack():
        for c in orders:
            c.wait_recv()
        labs = jnp.concatenate([ots[0]] + [otr[d] for d in range(1, nq)], axis=1)
        target = ((labs[2:3, :] - 1.0) * CAP + labs[1:2, :] - 1.0).astype(I32)

        def one(e, _):
            hit = iota((CAP, n * slots), 0) + e * CAP == target
            repack[e] = jnp.where(hit, 1.0, 0.0).astype(BF16)
            return 0

        lax.fori_loop(0, group, one, 0)

    directs = []
    spans = [list(range(k, min(k + 2, chunks))) for k in range(0, chunks, 2)]
    below = iota((half, CAP), 0) + half > iota((half, CAP), 1)

    def arrived(span):
        if span[0] == 0:
            make_repack()
        for k in span:
            for c in planes[k] if k < lined else directs:
                c.wait_recv()
        blocks = [plane[k].reshape(n * slots, width) for k in span]
        return blocks[0] if len(blocks) == 1 else jnp.concatenate(blocks, axis=1)

    def partial_gram(m):
        return lax.dot_general(m, m, (((1,), (1,)), ((), ())), preferred_element_type=F32)

    def add_gram(span):
        block = arrived(span)
        got = jnp.dot(repack[...].reshape(group * CAP, n * slots), block, preferred_element_type=F32)
        units[:, :, :block.shape[1]] = got.astype(BF16).reshape(group, CAP, block.shape[1])
        for e in range(group):
            s = partial_gram(units[e, :, :block.shape[1]])
            gram[e] = s if span[0] == 0 else gram[e] + s

    done = 0
    for k in range(lined):
        for c in lines[k]:
            c.wait_recv()
        if k + WINDOW < lined:
            send_line(k + WINDOW)
        if DIRECT and k == max(lined - 2, 0):
            for d in range(1, n):
                dz, dq = divmod(d, nq)
                directs.append(copy(straight.at[jnp.bitwise_xor(z, dz), dq],
                                    plane.at[chunks - 1, dq, pl.ds(dz * slots, slots)],
                                    s_dir.at[d], r_dir.at[d],
                                    jnp.bitwise_xor(z, dz) * nq + jnp.bitwise_xor(q, dq)))
            for c in directs:
                c.start()
        for d in range(nz):
            got = jnp.dot(pick[d], line[k, d], preferred_element_type=F32).astype(BF16)
            plane[k, 0, d * slots:(d + 1) * slots] = got[:slots]
            packed[k, :, d * slots:(d + 1) * slots] = got[slots:].reshape(nq - 1, slots, width)
        now = [copy(packed.at[k, d - 1], plane.at[k, d], s_plane.at[k, d], r_plane.at[k, d], on_plane(d))
               for d in range(nq - 1, 0, -1)]
        for c in now:
            c.start()
        planes.append(now)
        if done < len(spans) - 1 and spans[done][-1] + LAG <= k:
            add_gram(spans[done])
            done += 1
    while done < len(spans) - 1:
        add_gram(spans[done])
        done += 1

    block = arrived(spans[-1])
    wide = block.shape[1]
    halves = []
    for d in list(range(nz - 1, 0, -1)) + [0]:
        first = jnp.bitwise_xor(z, d) * per_owner
        got = jnp.dot(repack[pl.ds(first, per_owner)].reshape(per_owner * CAP, n * slots), block,
                      preferred_element_type=F32).astype(BF16)
        for l in range(per_owner):
            full = partial_gram(got[l * CAP:(l + 1) * CAP])
            if len(spans) > 1:
                full = full + gram[first + l]
            part = jnp.where(below, full[half:, :], pltpu.roll(full[:half, :], half, 1))
            if d:
                hs[d, l] = jnp.round(part * FIXED).astype(I32).astype(I16)
            else:
                own_half[l] = part
        if d:
            c = copy(hs.at[d], hr.at[d], s_h.at[d], r_h.at[d], on_line(d))
            c.start()
            halves.append(c)
    for group_of in [metas, orders, directs] + lines + planes:
        for c in group_of:
            c.wait_send()

    lane = iota((1, CAP), 1)
    at = jnp.where(lane < half, lane + half, lane - half).astype(F32)
    up_row = iota((half, CAP), 0)
    up_col = iota((half, CAP), 1)
    mine = [(me * per_owner + l).astype(F32) for l in range(per_owner)]
    n_mem = [jnp.sum(jnp.where(work_c == m, size_c, 0.0), axis=0, keepdims=True) for m in mine]
    for c in halves:
        c.wait_recv()
    bests, means = [], []
    for l in range(per_owner):
        far = hr[1, l].astype(I32)
        for d in range(2, nz):
            far = far + hr[d, l].astype(I32)
        p = own_half[l] + far.astype(F32) * (1.0 / FIXED)
        low = jnp.max(jnp.where(below & (up_col.astype(F32) < n_mem[l]), p, -1.0), axis=1, keepdims=True)
        low = jnp.max(jnp.where(up_row == up_col, low, -1.0), axis=0, keepdims=True)
        top_ok = (up_row + half < up_col) & (up_row.astype(F32) < n_mem[l])
        top = jnp.max(jnp.where(top_ok, p, -1.0), axis=0, keepdims=True)
        near = jnp.where(lane < half, low, top)
        live = at < n_mem[l]
        bests.append(jnp.where(live, near, -1.0))
        means.append(jnp.sum(jnp.where(live, near, 0.0), axis=1, keepdims=True) / n_mem[l])
    lanes = jnp.zeros((1, CAP), F32)
    for l in range(per_owner):
        lanes = jnp.where(lane == l, means[l], lanes)
    table[me] = rows_of(bests + [lanes], CAP)[:table.shape[1], :]
    backs = [copy(table.at[me], table.at[me], s_t.at[d], r_t.at[d], jnp.bitwise_xor(me, d))
             for d in range(n - 1, 0, -1)]
    for c in backs:
        c.start()
    pos = order[...]
    pos = jnp.where(pos < half, pos + half, pos - half)
    hot = jnp.where(iota((clusters, rows), 0) == work_row, 1.0, 0.0)
    for c in halves:
        c.wait_send()
    for c in backs:
        c.wait_recv()
    full = table[...]
    flat = full[:, :per_owner, :].reshape(clusters, CAP).T
    told = full[:, per_owner:per_owner + 1, :].reshape(n, CAP)
    mean = jnp.zeros((1, rows), F32)
    for l in range(per_owner):
        work = jnp.sum(jnp.where(slot_c == mine[l], work_c, 0.0), axis=0, keepdims=True).astype(I32)
        hit = iota((n, CAP), 0) * per_owner + iota((n, CAP), 1) == work
        hit = hit & (iota((n, CAP), 1) < per_owner)
        part = jnp.sum(jnp.where(hit, told, 0.0), axis=1, keepdims=True)
        mean = jnp.where(iota((1, rows), 1) == l, jnp.sum(part, axis=0, keepdims=True), mean)
    got = jnp.dot(flat, hot, preferred_element_type=F32, precision=lax.Precision.HIGHEST)
    out = jnp.sum(jnp.where(iota((CAP, rows), 0) == pos, got, 0.0), axis=0, keepdims=True)
    packed_out[...] = rows_of([out, mean], rows)
    for c in backs:
        c.wait_send()


def finish(packed, best_out, keep_out, mean_out):
    best = packed[0:1, :]
    best_out[...] = best
    keep_out[...] = jnp.where(best < CUTOFF, 1, 0)
    mean_out[...] = packed[1:2, :mean_out.shape[1]]


def body(embeddings, cluster_id, member_order, cluster_slot, cluster_size):
    n = lax.axis_size("dev")
    nz, nq = split_lines(n)
    rows, depth = embeddings.shape
    clusters = cluster_slot.shape[0]
    per_owner = clusters // n
    width = min(CHUNK, depth // nz)
    chunks = depth // nz // width
    group = nz * per_owner
    slots = source_slots(n, nq, rows, group)
    half = CAP // 2
    vmem = pl.BlockSpec(memory_space=pltpu.VMEM)
    dma = pltpu.SemaphoreType.DMA
    packed = pl.pallas_call(
        functools.partial(kernel, n, nz, nq),
        out_shape=jax.ShapeDtypeStruct((8, rows), F32),
        in_specs=[pl.BlockSpec(memory_space=pl.ANY)] * 5,
        out_specs=vmem,
        scratch_shapes=[
            pltpu.VMEM((rows, depth), F32),
            pltpu.VMEM((1, rows), I32),
            pltpu.VMEM((1, rows), I32),
            pltpu.VMEM((1, clusters), I32),
            pltpu.VMEM((1, clusters), I32),
            pltpu.VMEM((nz, chunks, rows, width), BF16),
            pltpu.VMEM((chunks, nz, rows, width), BF16),
            pltpu.VMEM((nz, 8, rows), F32),
            pltpu.VMEM((nz, nq * slots, rows), BF16),
            pltpu.VMEM((chunks, nq - 1, nz * slots, width), BF16),
            pltpu.VMEM((chunks, nq, nz * slots, width), BF16),
            pltpu.VMEM((nz, nq, slots, width), BF16),
            pltpu.VMEM((nq, 8, nz * slots), F32),
            pltpu.VMEM((nq, 8, nz * slots), F32),
            pltpu.VMEM((group, CAP, CAP), F32),
            pltpu.VMEM((per_owner, half, CAP), F32),
            pltpu.VMEM((nz, per_owner, half, CAP), I16),
            pltpu.VMEM((nz, per_owner, half, CAP), I16),
            pltpu.VMEM((n, pl.next_power_of_2(per_owner + 1), CAP), F32),
            pltpu.VMEM((group, CAP, 2 * width), BF16),
            pltpu.VMEM((group, CAP, n * slots), BF16),
            dma((LOADS,)), dma((4,)),
            dma((nz,)), dma((nz,)),
            dma((chunks, nz)), dma((chunks, nz)),
            dma((chunks, nq)), dma((chunks, nq)),
            dma((n,)), dma((n,)),
            dma((nq,)), dma((nq,)),
            dma((nz,)), dma((nz,)),
            dma((n,)), dma((n,)),
        ],
        compiler_params=pltpu.CompilerParams(
            collective_id=0, has_side_effects=True, vmem_limit_bytes=62 * 1024 * 1024),
    )(embeddings, cluster_id.reshape(1, rows), member_order.reshape(1, rows),
      cluster_slot.reshape(1, clusters), cluster_size.reshape(1, clusters))
    best, keep, mean = pl.pallas_call(
        finish,
        out_shape=(jax.ShapeDtypeStruct((1, rows), F32), jax.ShapeDtypeStruct((1, rows), I32),
                   jax.ShapeDtypeStruct((1, per_owner), F32)),
        in_specs=[vmem],
        out_specs=(vmem,) * 3,
    )(packed)
    return best.reshape(rows), keep.reshape(rows), mean.reshape(per_owner)


def solution(mesh):
    placed = (P(("rep", "dev"), None), P(("rep", "dev")), P(("rep", "dev")), P("rep"), P("rep"))
    return jax.shard_map(
        body,
        mesh=mesh,
        in_specs=placed,
        out_specs=(P(("rep", "dev")), P(("rep", "dev")), P(("rep", "dev"))),
        check_vma=False,
    )
```

time: 54.3 us -> 48.5 us (0.89)
  Pallas kernels: 53.5 us -> 47.7 us
    pallas_call x1, Pallas kernels: 52.3 us -> 46.5 us  [body(): pl.pallas_call(functools.partial(kernel, n, nz, nq), out_shape=jax.ShapeD...]
where the time goes in v1:
time: 48.5 us; the launch traced here: 48.3 us
  Pallas kernels  47.7 us (98%)
  between operations  0.64 us (1%)
    pallas_call x1, Pallas kernels, body(): pl.pallas_call(functools.partial(kernel, n, nz, nq), out_shape=jax.ShapeD...  46.5 us
    pallas_call x1, Pallas kernels, body(): pl.pallas_call(finish, out_shape=(jax.ShapeDtypeStruct((1, rows), F32), j...  1.19 us

profile of v1, /device:TPU:0, one launch (start us, length us, event | category | flops | bytes accessed | tf_op | source)
XLA Modules:
  0.0 48.3 jit_solution(10849220313358578650)
XLA Ops:
  0.6 46.5 %shard_map.76.packed = f32[8,128]{1,0:T(8,128)} custom-call(f32[128,4096]{1,0:T(8,128)} %emb_hbm.1, s32[1,128]{1,0:T(1,128)} %bitcast.7, s32[1,128]{1,0:T(1,128)} %bitcast.8, s32[1,32]{1,0:T(1,128)} %bitcast.9, s32[1,32]{1,0:T(1,128)} %bitcast.10), custom_call_target="tpu_custom_call" | custom-call | tf_op jit(solution)/shard_map/pallas_call | solution.py:347
  47.1 1.2 %shard_map.77 = (f32[1,128]{1,0:T(1,128)}, s32[1,128]{1,0:T(1,128)}, f32[1,2]{1,0:T(1,128)}) custom-call(f32[8,128]{1,0:T(8,128)} %shard_map.76.packed), custom_call_target="tpu_custom_call" | custom-call | tf_op jit(solution)/shard_map/pallas_call | solution.py:387

commit v2 on v1

v2 whole, which is shorter than its diff:
```python
import functools

import jax
import jax.numpy as jnp
from jax import lax
from jax.experimental import pallas as pl
from jax.experimental.pallas import tpu as pltpu
from jax.sharding import PartitionSpec as P

CAP = 128
CHUNK = 128
LOADS = 4
FAR_AHEAD = 4
SLOW = 2
LAG = 2
STRAIGHT = 1
NORM_EPS = 1e-06
CUTOFF = 0.8
META, ORDER, LINE, PLANE, DIRECT, HALF, BACK = range(7)
FIXED = 32000.0
F32 = jnp.float32
BF16 = jnp.bfloat16
I16 = jnp.int16
I32 = jnp.int32


def split_lines(n):
    z = max(z for z in range(1, n + 1) if n % z == 0 and z * z <= n)
    return z, n // z


def source_slots(n, nq, rows, group):
    largest = rows * n // nq + CAP - CAP // nq
    bound = (largest + group * (n - 1)) // n
    return min(group * -(-CAP // n), -(-bound // 16) * 16)


def iota(shape, dim):
    return lax.broadcasted_iota(I32, shape, dim)


def rows_of(values, width):
    row = iota((8, width), 0)
    out = jnp.zeros((8, width), values[0].dtype)
    for r, v in enumerate(values):
        out = jnp.where(row == r, jnp.broadcast_to(v, (8, width)), out)
    return out


def to_col(row, count):
    eye = iota((count, count), 0) == iota((count, count), 1)
    return jnp.sum(jnp.where(eye, row, 0.0), axis=1, keepdims=True)


def floor_div(x, d):
    return jnp.floor((x + 0.5) * (1.0 / d))


def kernel(n, nz, nq, emb_hbm, cid_hbm, order_hbm, slot_hbm, size_hbm, packed_out,
           emb, cid, order, slot, size, unit, line, meta, pick, packed, plane, straight, ots, otr,
           acc, hs, hr, table, units, repack,
           s_load, s_small, r_line, r_plane, sent, came):
    me = lax.axis_index("dev")
    z, q = lax.div(me, nq), lax.rem(me, nq)

    def copy(src, dst, s, r, target):
        return pltpu.make_async_remote_copy(
            src_ref=src, dst_ref=dst, send_sem=s, recv_sem=r,
            device_id={"dev": target}, device_id_type=pl.DeviceIdType.MESH)

    def arrive(ref, sem):
        pltpu.make_async_copy(ref, ref, sem).wait()

    def on_line(d):
        return jnp.bitwise_xor(z, d) * nq + q

    def on_plane(d):
        return z * nq + jnp.bitwise_xor(q, d)

    barrier = pltpu.get_barrier_semaphore()
    friends = [on_line(d) for d in range(1, nz)] + [on_plane(d) for d in range(1, nq)]
    for t in friends:
        pl.semaphore_signal(barrier, inc=1, device_id={"dev": t},
                            device_id_type=pl.DeviceIdType.MESH)
    smalls = [pltpu.make_async_copy(a, b, s_small.at[i]) for i, (a, b) in enumerate(
        [(cid_hbm, cid), (order_hbm, order), (slot_hbm, slot), (size_hbm, size)])]
    parts = s_load.shape[0]
    tall = emb.shape[0] // parts
    loads = [pltpu.make_async_copy(emb_hbm.at[pl.ds(i * tall, tall)], emb.at[pl.ds(i * tall, tall)],
                                   s_load.at[i]) for i in range(parts)]
    for c in smalls + loads:
        c.start()
    rows = emb.shape[0]
    clusters = slot.shape[1]
    per_owner = clusters // n
    chunks, width = line.shape[0], line.shape[3]
    group = nz * per_owner
    per_hub = group // 2
    first_hub = nz // 2 - 1
    slots = plane.shape[2] // nz
    half = CAP // 2
    lined = chunks - STRAIGHT

    for c in smalls:
        c.wait()
    slot_c = to_col(slot[...].astype(F32), clusters)
    size_r = size[...].astype(F32)
    size_c = to_col(size_r, clusters)
    c_row, c_col = iota((clusters, clusters), 1), iota((clusters, clusters), 0)
    ahead = (size_r > size_c) | ((size_r == size_c) & (c_row < c_col))
    place_in = jnp.sum(jnp.where(ahead, 1.0, 0.0), axis=1, keepdims=True)
    e_c = floor_div(place_in, nq)
    turn = place_in - e_c * nq
    odd = e_c - 2.0 * floor_div(e_c, 2)
    g_c = jnp.where(odd > 0.5, nq - 1 - turn, turn)
    hub_c = floor_div(e_c, per_hub)
    work_c = (hub_c * nq + g_c) * per_hub + e_c - hub_c * per_hub
    is_mem = iota((clusters, rows), 0) == cid[...]

    def of_row(v):
        return jnp.sum(jnp.where(is_mem, v, 0.0), axis=0, keepdims=True)

    e_row, work_row = of_row(e_c), of_row(work_c).astype(I32)
    rel = jnp.bitwise_xor(of_row(g_c).astype(I32), q)
    tri = (iota((rows, rows), 0) < iota((rows, rows), 1)).astype(F32).astype(BF16)
    wide_q = -(-nq // 16) * 16
    in_group = iota((wide_q, rows), 0) == rel
    before = jnp.dot(in_group.astype(F32).astype(BF16), tri, preferred_element_type=F32)
    rank = jnp.sum(jnp.where(in_group, before, 0.0), axis=0, keepdims=True)
    place = rel.astype(F32) * slots + rank
    ord_row = order[...].astype(F32)
    meta[0] = rows_of([place, ord_row + 1.0, e_row + 1.0], rows)

    sums = []
    for i in range(parts):
        loads[i].wait()
        x = emb[i * tall:(i + 1) * tall, :]
        sums.append(jnp.sum(x * x, axis=1, keepdims=True))
    scale = lax.rsqrt(jnp.concatenate(sums, axis=0) + NORM_EPS)

    line_order = [d for d in (2, 3, 1) if d < nz] + list(range(4, nz))

    def make_unit(k):
        for t in range(nz):
            c0 = (t * chunks + k) * width
            unit[t, k] = (emb[:, c0:c0 + width] * scale).astype(BF16)

    def send_line(k):
        for d in line_order:
            copy(unit.at[jnp.bitwise_xor(z, d), k], line.at[k, d], sent.at[LINE], r_line.at[k], on_line(d)).start()
        line[k, 0] = unit[z, k]

    pl.semaphore_wait(barrier, len(friends))
    for d in range(1, nz):
        copy(meta.at[0], meta.at[d], sent.at[META], came.at[META], on_line(d)).start()
    far = lax.axis_index("rep") == 0
    for k in range(chunks):
        make_unit(k)
        if k < min(FAR_AHEAD, lined):
            pl.when(far | (k == 0))(functools.partial(send_line, k))
    def label(d):
        pick[d] = jnp.where(iota((nq * slots, rows), 0) == meta[d, 0:1, :].astype(I32), 1.0, 0.0).astype(BF16)
        values = jnp.where((iota((8, rows), 0) == 1) | (iota((8, rows), 0) == 2), meta[d], 0.0).astype(BF16)
        return lax.dot_general(values, pick[d], (((1,), (1,)), ((), ())), preferred_element_type=F32)

    told = [label(0)]
    if STRAIGHT:
        for t in range(nz):
            got = jnp.dot(pick[0], unit[t, chunks - 1], preferred_element_type=F32).astype(BF16)
            straight[t * nq:(t + 1) * nq] = got.reshape(nq, slots, width)
        plane[chunks - 1, 0, 0:slots] = straight[z * nq]
    arrive(meta.at[pl.ds(1, nz - 1)], came.at[META])
    told += [label(d) for d in range(1, nz)]
    for d in range(nq):
        ots[d] = jnp.concatenate([v[:, d * slots:(d + 1) * slots] for v in told], axis=1)
    for d in range(1, nq):
        copy(ots.at[d], otr.at[d], sent.at[ORDER], came.at[ORDER], on_plane(d)).start()

    def make_repack():
        arrive(otr.at[pl.ds(1, nq - 1)], came.at[ORDER])
        labs = jnp.concatenate([ots[0]] + [otr[d] for d in range(1, nq)], axis=1)
        target = ((labs[2:3, :] - 1.0) * CAP + labs[1:2, :] - 1.0).astype(I32)

        def one(e, _):
            hit = iota((CAP, n * slots), 0) + e * CAP == target
            repack[e] = jnp.where(hit, 1.0, 0.0).astype(BF16)
            return 0

        lax.fori_loop(0, group, one, 0)

    pair = 2 if chunks % 2 == 0 else 1
    spans = chunks // pair
    below = iota((half, CAP), 0) + half > iota((half, CAP), 1)
    acc[...] = jnp.zeros(acc.shape, F32)

    def take_line(k):
        arrive(line.at[k, pl.ds(1, nz - 1)], r_line.at[k])

        @pl.when(jnp.logical_not(far) & (k == SLOW) & (k + 1 < lined))
        def _():
            send_line(k + 1)

        ahead = jnp.where(far, FAR_AHEAD, jnp.where(k < SLOW, 1, 2))

        @pl.when(k + ahead < lined)
        def _():
            send_line(k + ahead)

        if STRAIGHT:
            @pl.when(k == max(lined - 3, 0))
            def _():
                for d in range(1, n):
                    dz, dq = divmod(d, nq)
                    copy(straight.at[jnp.bitwise_xor(z, dz) * nq + dq],
                         plane.at[chunks - 1, dq, pl.ds(dz * slots, slots)],
                         sent.at[DIRECT], came.at[DIRECT], jnp.bitwise_xor(z, dz) * nq + jnp.bitwise_xor(q, dq)).start()

        for d in range(nz):
            got = jnp.dot(pick[d], line[k, d], preferred_element_type=F32).astype(BF16)
            plane[k, 0, d * slots:(d + 1) * slots] = got[:slots]
            packed[k, :, d * slots:(d + 1) * slots] = got[slots:].reshape(nq - 1, slots, width)
        for d in range(nq - 1, 0, -1):
            copy(packed.at[k, d - 1], plane.at[k, d], sent.at[PLANE], r_plane.at[k], on_plane(d)).start()

    def take_span(j):
        for i in range(pair):
            k = j * pair + i

            @pl.when(k < lined)
            def _():
                arrive(plane.at[k, pl.ds(1, nq - 1)], r_plane.at[k])

            if STRAIGHT:
                @pl.when(k == lined)
                def _():
                    arrive(straight.at[pl.ds(1, n - 1)], came.at[DIRECT])
        block = [plane[j * pair + i].reshape(n * slots, width) for i in range(pair)]
        block = jnp.concatenate(block, axis=1) if pair > 1 else block[0]
        got = jnp.dot(repack[...].reshape(group * CAP, n * slots), block, preferred_element_type=F32)
        units[...] = got.astype(BF16).reshape(units.shape)

        for b in range(group // 2):
            m = units[b]
            s = lax.dot_general(m, m, (((1,), (1,)), ((), ())), preferred_element_type=F32)
            for l in range(2):
                full = s[l * CAP:(l + 1) * CAP, l * CAP:(l + 1) * CAP]
                part = acc[2 * b + l] + jnp.where(below, full[half:, :], pltpu.roll(full[:half, :], half, 1))
                acc[2 * b + l] = part
                hs[2 * b + l] = jnp.round(part * FIXED).astype(I32).astype(I16)

        @pl.when(j == spans - 1)
        def _():
            for i in range(2):
                h = jnp.where(z > first_hub, i, 1 - i)

                @pl.when(z != first_hub + h)
                def _():
                    copy(hs.at[pl.ds(h * per_hub, per_hub)], hr.at[jnp.bitwise_xor(z, first_hub + h)],
                         sent.at[HALF], came.at[HALF], (first_hub + h) * nq + q).start()

    def step(k, _):
        @pl.when(k < lined)
        def _():
            take_line(k)

        @pl.when(k == min(lined, pair + LAG - 1) - 1)
        def _():
            make_repack()

        back = k - LAG - (pair - 1)

        @pl.when((back >= 0) & (lax.rem(back, pair) == 0))
        def _():
            take_span(lax.div(back, pair))
        return 0

    lax.fori_loop(0, pair * spans + LAG, step, 0)
    arrive(meta.at[pl.ds(1, nz - 1)], sent.at[META])
    arrive(ots.at[pl.ds(1, nq - 1)], sent.at[ORDER])
    arrive(line.at[pl.ds(0, lined), pl.ds(1, nz - 1)], sent.at[LINE])
    arrive(packed.at[pl.ds(0, lined)], sent.at[PLANE])
    if STRAIGHT:
        arrive(straight.at[pl.ds(1, n - 1)], sent.at[DIRECT])

    lane = iota((1, CAP), 1)
    at = jnp.where(lane < half, lane + half, lane - half).astype(F32)
    up_row = iota((half, CAP), 0)
    up_col = iota((half, CAP), 1)
    is_hub = (z == first_hub) | (z == first_hub + 1)
    hub = (z - first_hub) * nq + q

    @pl.when(is_hub)
    def _():
        own = (z - first_hub) * per_hub
        n_mem = []
        for l in range(per_hub):
            w = (hub * per_hub + l).astype(F32)
            n_mem.append(jnp.sum(jnp.where(work_c == w, size_c, 0.0), axis=0, keepdims=True))
        arrive(hr.at[pl.ds(1, nz - 1)], came.at[HALF])
        for l in range(per_hub):
            apart = hr[1, l].astype(I32)
            for d in range(2, nz):
                apart = apart + hr[d, l].astype(I32)
            p = acc[own + l] + apart.astype(F32) * (1.0 / FIXED)
            low = jnp.max(jnp.where(below & (up_col.astype(F32) < n_mem[l]), p, -1.0), axis=1, keepdims=True)
            low = jnp.max(jnp.where(up_row == up_col, low, -1.0), axis=0, keepdims=True)
            top_ok = (up_row + half < up_col) & (up_row.astype(F32) < n_mem[l])
            top = jnp.max(jnp.where(top_ok, p, -1.0), axis=0, keepdims=True)
            live = at < n_mem[l]
            near = jnp.where(live, jnp.where(lane < half, low, top), -1.0)
            mean = jnp.sum(jnp.where(live, near, 0.0), axis=1, keepdims=True) / n_mem[l]
            table[hub, l:l + 1] = jnp.where(lane == half, mean, near)
        for d in range(n - 1, 0, -1):
            copy(table.at[hub], table.at[hub], sent.at[BACK], came.at[BACK], jnp.bitwise_xor(me, d)).start()

    pos = order[...]
    pos = jnp.where(pos < half, pos + half, pos - half)
    hot = jnp.where(iota((clusters, rows), 0) == work_row, 1.0, 0.0)
    hubs = table.shape[0]

    @pl.when(is_hub)
    def _():
        arrive(hs.at[pl.ds(0, per_hub)], sent.at[HALF])
        arrive(table.at[pl.ds(0, hubs - 1)], came.at[BACK])

    @pl.when(jnp.logical_not(is_hub))
    def _():
        arrive(hs, sent.at[HALF])
        arrive(table, came.at[BACK])

    flat = table[...].reshape(clusters, CAP)
    mean = jnp.zeros((1, rows), F32)
    for l in range(per_owner):
        work = jnp.sum(jnp.where(slot_c == (me * per_owner + l).astype(F32), work_c, 0.0), axis=0, keepdims=True).astype(I32)
        hit = (iota((clusters, CAP), 0) == work) & (iota((clusters, CAP), 1) == half)
        part = jnp.sum(jnp.where(hit, flat, 0.0), axis=1, keepdims=True)
        mean = jnp.where(iota((1, rows), 1) == l, jnp.sum(part, axis=0, keepdims=True), mean)
    got = jnp.dot(flat.T, hot, preferred_element_type=F32, precision=lax.Precision.HIGHEST)
    out = jnp.sum(jnp.where(iota((CAP, rows), 0) == pos, got, 0.0), axis=0, keepdims=True)
    out = jnp.where(order[...] == 0, -1.0, out)
    packed_out[...] = rows_of([out, mean], rows)
    @pl.when(is_hub)
    def _():
        for d in range(0, n - 1, hubs - 1):
            arrive(table.at[pl.ds(0, min(hubs - 1, n - 1 - d))], sent.at[BACK])


def finish(packed, best_out, keep_out, mean_out):
    best = packed[0:1, :]
    best_out[...] = best
    keep_out[...] = jnp.where(best < CUTOFF, 1, 0)
    mean_out[...] = packed[1:2, :mean_out.shape[1]]


def body(embeddings, cluster_id, member_order, cluster_slot, cluster_size):
    n = lax.axis_size("dev")
    nz, nq = split_lines(n)
    rows, depth = embeddings.shape
    clusters = cluster_slot.shape[0]
    per_owner = clusters // n
    width = min(CHUNK, depth // nz)
    chunks = depth // nz // width
    group = nz * per_owner
    slots = source_slots(n, nq, rows, group)
    pair = 2 if chunks % 2 == 0 else 1
    half = CAP // 2
    vmem = pl.BlockSpec(memory_space=pltpu.VMEM)
    dma = pltpu.SemaphoreType.DMA
    packed = pl.pallas_call(
        functools.partial(kernel, n, nz, nq),
        out_shape=jax.ShapeDtypeStruct((8, rows), F32),
        in_specs=[pl.BlockSpec(memory_space=pl.ANY)] * 5,
        out_specs=vmem,
        scratch_shapes=[
            pltpu.VMEM((rows, depth), F32),
            pltpu.VMEM((1, rows), I32),
            pltpu.VMEM((1, rows), I32),
            pltpu.VMEM((1, clusters), I32),
            pltpu.VMEM((1, clusters), I32),
            pltpu.VMEM((nz, chunks, rows, width), BF16),
            pltpu.VMEM((chunks, nz, rows, width), BF16),
            pltpu.VMEM((nz, 8, rows), F32),
            pltpu.VMEM((nz, nq * slots, rows), BF16),
            pltpu.VMEM((chunks, nq - 1, nz * slots, width), BF16),
            pltpu.VMEM((chunks, nq, nz * slots, width), BF16),
            pltpu.VMEM((n, slots, width), BF16),
            pltpu.VMEM((nq, 8, nz * slots), F32),
            pltpu.VMEM((nq, 8, nz * slots), F32),
            pltpu.VMEM((group, half, CAP), F32),
            pltpu.VMEM((group, half, CAP), I16),
            pltpu.VMEM((nz, group // 2, half, CAP), I16),
            pltpu.VMEM((2 * nq, group // 2, CAP), F32),
            pltpu.VMEM((group // 2, 2 * CAP, pair * width), BF16),
            pltpu.VMEM((group, CAP, n * slots), BF16),
            dma((LOADS,)), dma((4,)), dma((chunks,)), dma((chunks,)), dma((7,)), dma((7,)),
        ],
        compiler_params=pltpu.CompilerParams(
            collective_id=0, has_side_effects=True, vmem_limit_bytes=62 * 1024 * 1024),
    )(embeddings, cluster_id.reshape(1, rows), member_order.reshape(1, rows),
      cluster_slot.reshape(1, clusters), cluster_size.reshape(1, clusters))
    best, keep, mean = pl.pallas_call(
        finish,
        out_shape=(jax.ShapeDtypeStruct((1, rows), F32), jax.ShapeDtypeStruct((1, rows), I32),
                   jax.ShapeDtypeStruct((1, per_owner), F32)),
        in_specs=[vmem],
        out_specs=(vmem,) * 3,
    )(packed)
    return best.reshape(rows), keep.reshape(rows), mean.reshape(per_owner)


def solution(mesh):
    placed = (P(("rep", "dev"), None), P(("rep", "dev")), P(("rep", "dev")), P("rep"), P("rep"))
    return jax.shard_map(
        body,
        mesh=mesh,
        in_specs=placed,
        out_specs=(P(("rep", "dev")), P(("rep", "dev")), P(("rep", "dev"))),
        check_vma=False,
    )
```

time: 48.5 us -> 43.6 us (0.90)
  the two profiles are of different devices: /device:TPU:0 before, /device:TPU:1 now
where the time goes in v2:
time: 43.6 us; the launch traced here: 43.4 us
  Pallas kernels  42.8 us (98%)
  between operations  0.64 us (1%)
    pallas_call x1, Pallas kernels, body(): pl.pallas_call(functools.partial(kernel, n, nz, nq), out_shape=jax.ShapeD...  41.6 us
    pallas_call x1, Pallas kernels, body(): pl.pallas_call(finish, out_shape=(jax.ShapeDtypeStruct((1, rows), F32), j...  1.19 us

profile of v2, /device:TPU:1, one launch (start us, length us, event | category | flops | bytes accessed | tf_op | source)
XLA Modules:
  0.0 43.4 jit_solution(9993351094765057205)
XLA Ops:
  0.6 41.6 %shard_map.76.packed = f32[8,128]{1,0:T(8,128)} custom-call(f32[128,4096]{1,0:T(8,128)} %emb_hbm.1, s32[1,128]{1,0:T(1,128)} %bitcast.7, s32[1,128]{1,0:T(1,128)} %bitcast.8, s32[1,32]{1,0:T(1,128)} %bitcast.9, s32[1,32]{1,0:T(1,128)} %bitcast.10), custom_call_target="tpu_custom_call" | custom-call | tf_op jit(solution)/shard_map/pallas_call | solution.py:369
  42.2 1.2 %shard_map.77 = (f32[1,128]{1,0:T(1,128)}, s32[1,128]{1,0:T(1,128)}, f32[1,2]{1,0:T(1,128)}) custom-call(f32[8,128]{1,0:T(8,128)} %shard_map.76.packed), custom_call_target="tpu_custom_call" | custom-call | tf_op jit(solution)/shard_map/pallas_call | solution.py:401

commit v3 on v2

--- a/solution.py
+++ b/solution.py
@@ -368,7 +368,7 @@
     dma = pltpu.SemaphoreType.DMA
     packed = pl.pallas_call(
         functools.partial(kernel, n, nz, nq),
-        out_shape=jax.ShapeDtypeStruct((8, rows), F32),
+        out_shape=pltpu.VMEM((8, rows), F32),
         in_specs=[pl.BlockSpec(memory_space=pl.ANY)] * 5,
         out_specs=vmem,
         scratch_shapes=[
@@ -404,7 +404,7 @@
                    jax.ShapeDtypeStruct((1, per_owner), F32)),
         in_specs=[vmem],
         out_specs=(vmem,) * 3,
-    )(packed)
+    )(pltpu.with_memory_space_constraint(packed, pltpu.VMEM))
     return best.reshape(rows), keep.reshape(rows), mean.reshape(per_owner)
 
 

time: 43.6 us -> 42.3 us (0.970)
  Pallas kernels: 42.8 us -> 41.5 us
    pallas_call x1, Pallas kernels: 1.19 us -> 0.52 us  [body(): pl.pallas_call(finish, out_shape=(jax.ShapeDtypeStruct((1, rows), F32), j...]
    pallas_call x1, Pallas kernels: 41.6 us -> 41 us  [body(): pl.pallas_call(functools.partial(kernel, n, nz, nq), out_shape=pltpu.VMEM...]
where the time goes in v3:
time: 42.3 us; the launch traced here: 42.2 us
  Pallas kernels  41.5 us (98%)
  between operations  0.64 us (2%)
    pallas_call x1, Pallas kernels, body(): pl.pallas_call(functools.partial(kernel, n, nz, nq), out_shape=pltpu.VMEM...  41 us

profile of v3, /device:TPU:1, one launch (start us, length us, event | category | flops | bytes accessed | tf_op | source)
XLA Modules:
  0.0 42.2 jit_solution(622040669544954540)
XLA Ops:
  0.6 41.0 %shard_map.76.packed = f32[8,128]{1,0:T(8,128)S(1)} custom-call(f32[128,4096]{1,0:T(8,128)} %emb_hbm.1, s32[1,128]{1,0:T(1,128)} %bitcast.7, s32[1,128]{1,0:T(1,128)} %bitcast.8, s32[1,32]{1,0:T(1,128)} %bitcast.9, s32[1,32]{1,0:T(1,128)} %bitcast.10), custom_call_target="tpu_custom_call" | custom-call | tf_op jit(solution)/shard_map/pallas_call | solution.py:369
  41.6 0.5 %shard_map.77 = (f32[1,128]{1,0:T(1,128)}, s32[1,128]{1,0:T(1,128)}, f32[1,2]{1,0:T(1,128)}) custom-call(f32[8,128]{1,0:T(8,128)S(1)} %shard_map.76.packed), custom_call_target="tpu_custom_call" | custom-call | tf_op jit(solution)/shard_map/pallas_call | solution.py:401

commit v4 on v3

--- a/solution.py
+++ b/solution.py
@@ -138,7 +138,7 @@
         sums.append(jnp.sum(x * x, axis=1, keepdims=True))
     scale = lax.rsqrt(jnp.concatenate(sums, axis=0) + NORM_EPS)
 
-    line_order = [d for d in (2, 3, 1) if d < nz] + list(range(4, nz))
+    line_order = [d for d in (3, 2, 1) if d < nz] + list(range(4, nz))
 
     def make_unit(k):
         for t in range(nz):
@@ -239,24 +239,22 @@
         got = jnp.dot(repack[...].reshape(group * CAP, n * slots), block, preferred_element_type=F32)
         units[...] = got.astype(BF16).reshape(units.shape)
 
-        for b in range(group // 2):
-            m = units[b]
-            s = lax.dot_general(m, m, (((1,), (1,)), ((), ())), preferred_element_type=F32)
-            for l in range(2):
-                full = s[l * CAP:(l + 1) * CAP, l * CAP:(l + 1) * CAP]
-                part = acc[2 * b + l] + jnp.where(below, full[half:, :], pltpu.roll(full[:half, :], half, 1))
-                acc[2 * b + l] = part
-                hs[2 * b + l] = jnp.round(part * FIXED).astype(I32).astype(I16)
-
-        @pl.when(j == spans - 1)
-        def _():
-            for i in range(2):
-                h = jnp.where(z > first_hub, i, 1 - i)
-
-                @pl.when(z != first_hub + h)
-                def _():
-                    copy(hs.at[pl.ds(h * per_hub, per_hub)], hr.at[jnp.bitwise_xor(z, first_hub + h)],
-                         sent.at[HALF], came.at[HALF], (first_hub + h) * nq + q).start()
+        for i in range(2):
+            h = jnp.where(z > first_hub, i, 1 - i)
+            for e in range(0, per_hub, 2):
+                e = h * per_hub + e
+                m = units[lax.div(e, 2)]
+                s = lax.dot_general(m, m, (((1,), (1,)), ((), ())), preferred_element_type=F32)
+                for l in range(2):
+                    full = s[l * CAP:(l + 1) * CAP, l * CAP:(l + 1) * CAP]
+                    part = acc[e + l] + jnp.where(below, full[half:, :], pltpu.roll(full[:half, :], half, 1))
+                    acc[e + l] = part
+                    hs[e + l] = jnp.round(part * FIXED).astype(I32).astype(I16)
+
+            @pl.when((j == spans - 1) & (z != first_hub + h))
+            def _():
+                copy(hs.at[pl.ds(h * per_hub, per_hub)], hr.at[jnp.bitwise_xor(z, first_hub + h)],
+                     sent.at[HALF], came.at[HALF], (first_hub + h) * nq + q).start()
 
     def step(k, _):
         @pl.when(k < lined)
@@ -310,7 +308,7 @@
             near = jnp.where(live, jnp.where(lane < half, low, top), -1.0)
             mean = jnp.sum(jnp.where(live, near, 0.0), axis=1, keepdims=True) / n_mem[l]
             table[hub, l:l + 1] = jnp.where(lane == half, mean, near)
-        for d in range(n - 1, 0, -1):
+        for d in sorted(range(1, n), key=lambda d: d // nq in (0, nz - 1)):
             copy(table.at[hub], table.at[hub], sent.at[BACK], came.at[BACK], jnp.bitwise_xor(me, d)).start()
 
     pos = order[...]

time: 42.3 us -> 42 us (level)
  no operation moved by 1% of the time
where the time goes in v4:
time: 42 us; the launch traced here: 41.8 us
  Pallas kernels  41.2 us (98%)
  between operations  0.64 us (2%)
    pallas_call x1, Pallas kernels, body(): pl.pallas_call(functools.partial(kernel, n, nz, nq), out_shape=pltpu.VMEM...  40.7 us

profile of v4, /device:TPU:1, one launch (start us, length us, event | category | flops | bytes accessed | tf_op | source)
XLA Modules:
  0.0 41.8 jit_solution(6688551700725386849)
XLA Ops:
  0.6 40.7 %shard_map.76.packed = f32[8,128]{1,0:T(8,128)S(1)} custom-call(f32[128,4096]{1,0:T(8,128)} %emb_hbm.1, s32[1,128]{1,0:T(1,128)} %bitcast.7, s32[1,128]{1,0:T(1,128)} %bitcast.8, s32[1,32]{1,0:T(1,128)} %bitcast.9, s32[1,32]{1,0:T(1,128)} %bitcast.10), custom_call_target="tpu_custom_call" | custom-call | tf_op jit(solution)/shard_map/pallas_call | solution.py:367
  41.3 0.5 %shard_map.77 = (f32[1,128]{1,0:T(1,128)}, s32[1,128]{1,0:T(1,128)}, f32[1,2]{1,0:T(1,128)}) custom-call(f32[8,128]{1,0:T(8,128)S(1)} %shard_map.76.packed), custom_call_target="tpu_custom_call" | custom-call | tf_op jit(solution)/shard_map/pallas_call | solution.py:399

commit v5 on v4

--- a/solution.py
+++ b/solution.py
@@ -16,7 +16,7 @@
 STRAIGHT = 1
 NORM_EPS = 1e-06
 CUTOFF = 0.8
-META, ORDER, LINE, PLANE, DIRECT, HALF, BACK = range(7)
+META, ORDER, DIRECT, HALF, BACK, LINE, PLANE = range(7)
 FIXED = 32000.0
 F32 = jnp.float32
 BF16 = jnp.bfloat16
@@ -249,10 +249,11 @@
                     full = s[l * CAP:(l + 1) * CAP, l * CAP:(l + 1) * CAP]
                     part = acc[e + l] + jnp.where(below, full[half:, :], pltpu.roll(full[:half, :], half, 1))
                     acc[e + l] = part
-                    hs[e + l] = jnp.round(part * FIXED).astype(I32).astype(I16)
 
             @pl.when((j == spans - 1) & (z != first_hub + h))
             def _():
+                for l in range(per_hub):
+                    hs[h * per_hub + l] = jnp.round(acc[h * per_hub + l] * FIXED).astype(I32).astype(I16)
                 copy(hs.at[pl.ds(h * per_hub, per_hub)], hr.at[jnp.bitwise_xor(z, first_hub + h)],
                      sent.at[HALF], came.at[HALF], (first_hub + h) * nq + q).start()
 
@@ -390,7 +391,7 @@
             pltpu.VMEM((2 * nq, group // 2, CAP), F32),
             pltpu.VMEM((group // 2, 2 * CAP, pair * width), BF16),
             pltpu.VMEM((group, CAP, n * slots), BF16),
-            dma((LOADS,)), dma((4,)), dma((chunks,)), dma((chunks,)), dma((7,)), dma((7,)),
+            dma((LOADS,)), dma((4,)), dma((chunks - STRAIGHT,)), dma((chunks - STRAIGHT,)), dma((7,)), dma((5,)),
         ],
         compiler_params=pltpu.CompilerParams(
             collective_id=0, has_side_effects=True, vmem_limit_bytes=62 * 1024 * 1024),

time: 42 us -> 42 us (level)
  no operation moved by 1% of the time
where the time goes in v5:
time: 42 us; the launch traced here: 41.8 us
  Pallas kernels  41.2 us (98%)
  between operations  0.64 us (2%)
    pallas_call x1, Pallas kernels, body(): pl.pallas_call(functools.partial(kernel, n, nz, nq), out_shape=pltpu.VMEM...  40.6 us

profile of v5, /device:TPU:1, one launch (start us, length us, event | category | flops | bytes accessed | tf_op | source)
XLA Modules:
  0.0 41.8 jit_solution(7106208396494636151)
XLA Ops:
  0.6 40.6 %shard_map.76.packed = f32[8,128]{1,0:T(8,128)S(1)} custom-call(f32[128,4096]{1,0:T(8,128)} %emb_hbm.1, s32[1,128]{1,0:T(1,128)} %bitcast.7, s32[1,128]{1,0:T(1,128)} %bitcast.8, s32[1,32]{1,0:T(1,128)} %bitcast.9, s32[1,32]{1,0:T(1,128)} %bitcast.10), custom_call_target="tpu_custom_call" | custom-call | tf_op jit(solution)/shard_map/pallas_call | solution.py:368
  41.3 0.5 %shard_map.77 = (f32[1,128]{1,0:T(1,128)}, s32[1,128]{1,0:T(1,128)}, f32[1,2]{1,0:T(1,128)}) custom-call(f32[8,128]{1,0:T(8,128)S(1)} %shard_map.76.packed), custom_call_target="tpu_custom_call" | custom-call | tf_op jit(solution)/shard_map/pallas_call | solution.py:400
